TPU v7x, 32 devices: a whole 2x2x4 slice. The times are simulated.
32 devices in a mesh: fsdp: 16 (over z, y, core), tp: 2 (over x).
Axes of the slice: x: 2, y: 2, z: 4, core: 2. Of those that a mesh axis runs over, the one named last changes fastest.
Arguments:
- tokens: bfloat16 [6144, 5632], P('fsdp', 'tp'), may hold values from -6 to 6
- gain: float32 [5632], replicated, may hold values from 0.1 to 1.9
- query_projection_weight: bfloat16 [5632, 6144], P('fsdp', 'tp'), may hold values from -0.078125 to 0.078125
- key_projection_weight: bfloat16 [5632, 1024], P('fsdp', 'tp'), may hold values from -0.078125 to 0.078125
- value_projection_weight: bfloat16 [5632, 1024], P('fsdp', 'tp'), may hold values from -0.078125 to 0.078125
- adapter_down_factors: bfloat16 [3, 16, 5632], replicated, may hold values from -0.078125 to 0.078125
- query_adapter_up: bfloat16 [16, 6144], P(None, 'tp'), may hold values from -0.078125 to 0.078125
- key_adapter_up: bfloat16 [16, 1024], P(None, 'tp'), may hold values from -0.1875 to 0.1875
- value_adapter_up: bfloat16 [16, 1024], P(None, 'tp'), may hold values from -0.1875 to 0.1875
- query_cotangent: bfloat16 [6144, 6144], P('fsdp', 'tp'), may hold values from -6 to 6
- key_cotangent: bfloat16 [6144, 1024], P('fsdp', 'tp'), may hold values from -6 to 6
- value_cotangent: bfloat16 [6144, 1024], P('fsdp', 'tp'), may hold values from -6 to 6
Outputs:
- grad_tokens: bfloat16 [6144, 5632], P('fsdp', 'tp')
- grad_down: float32 [3, 16, 5632], P(None, None, 'tp')
- grad_up_query: float32 [16, 6144], P(None, 'tp')
- grad_up_key: float32 [16, 1024], P(None, 'tp')
- grad_up_value: float32 [16, 1024], P(None, 'tp')
All inputs are finite; a program needn't handle non-finite values.
Results may differ from a plain program's by a relative error of at most 0.0096.
Values may be sent and summed in bfloat16 or wider, within the bound.
A program may use at most 128 MiB of HBM per device.

v0:
```python
import functools
import math

import jax
import jax.numpy as jnp
from jax import lax
from jax.experimental import pallas as pl
from jax.experimental.pallas import tpu as pltpu
from jax.sharding import PartitionSpec as P

norm_eps = 1e-05
adapter_scale = 2.0


def transposed_product(left, right):
    return lax.dot_general(
        left, right, (((1,), (1,)), ((), ())), preferred_element_type=jnp.float32
    )


def plain_back(weights, cotangents, full_width):
    total = jnp.zeros((cotangents[0].shape[0], full_width), jnp.float32)
    for weight, cotangent in zip(weights, cotangents):
        whole = lax.all_gather(weight, "fsdp", axis=0, tiled=True)
        total = total + transposed_product(cotangent, whole)
    return lax.psum_scatter(total, "tp", scatter_dimension=1, tiled=True)


def near_and_far_orders(count):
    near = range(count)
    outer, outer_marks = [], {}
    inner, inner_marks = [], {}

    def add(order, marks, name, tiles):
        marks[name] = len(order)
        order.extend(tiles)

    def grid(ws, ts):
        return [(w, t) for w in ws for t in ts]

    add(outer, outer_marks, "near", grid((0, 1), near))
    add(outer, outer_marks, "f0", grid((4,), near))
    add(outer, outer_marks, "y", grid((2, 3), near))
    add(outer, outer_marks, "f1", grid((5,), near))
    done = [0, 1, 2, 3, 4, 5]
    for i in range(count):
        add(outer, outer_marks, f"z{i}", grid(done, (count + i,)))
        if i >= count - 3 and i < count - 1:
            w = 6 + i - (count - 3)
            add(outer, outer_marks, f"fy{w - 6}", grid((w,), range(count + i + 1)))
            done.append(w)
    every = range(2 * count)
    add(inner, inner_marks, "near", grid((0, 1), near))
    for i in range(count):
        add(inner, inner_marks, f"z{i}", grid((0, 1), (count + i,)))
    add(inner, inner_marks, "y", grid((2, 3), every))
    add(inner, inner_marks, "f0", grid((4,), every))
    add(inner, inner_marks, "fy0", grid((6,), every))
    add(inner, inner_marks, "f1", grid((5,), every))
    add(inner, inner_marks, "fy1", grid((7,), every))
    return (outer, outer_marks), (inner, inner_marks)


def packed(digits):
    words = []
    for low in range(0, len(digits), 10):
        words.append(sum(d << (3 * k) for k, d in enumerate(digits[low : low + 10])))
    return words


def digit_at(step, is_inner, outer_digits, inner_digits):
    word = jnp.int32(0)
    for k, (o, i) in enumerate(zip(packed(outer_digits), packed(inner_digits))):
        value = jnp.where(is_inner == 1, jnp.int32(i), jnp.int32(o))
        word = jnp.where(step // 10 == k, value, word)
    return lax.shift_right_logical(word, 3 * (step % 10)) % 8


def piece_rows(half):
    size = 48 if half > 48 else half
    cuts = list(range(0, half, size)) + [half]
    return list(zip(cuts[:-1], cuts[1:]))


def grid_kernel(
    settings,
    cq, ck, cv, wq, wk, wv, tokens, gain, adapters, uq, uk, uv,
    out, grad_down, grad_up_q, grad_up_k, grad_up_v,
    W, C, S, X, R,
    T, GA, U, D, GD, A, AR, INV, LO, ZT, N, B, I, IR,
    G, GC, GY, H, HZ, F,
    load_w, load_c, load_s,
    a_send, a_recv, i_send, i_recv,
    gc_send, gc_recv, gy_send, gy_recv, gz_send, gz_recv, ga_send, ga_recv, gb_send, gb_recv, gd_send, gd_recv,
    cc_send, cc_recv, cz_send, cz_recv, zc_send, zc_recv,
    y_send, y_recv, far_send, far_recv, fy_send, fy_recv,
    x_send, x_recv, r_send, r_recv,
):
    half = W.shape[1]
    block = 2 * half
    count = C.shape[0] // 2
    lanes = R.shape[2]
    top = 8
    place = lax.axis_index("fsdp")
    side = lax.axis_index("tp")

    def flipped(bit):
        return place + bit * (1 - 2 * ((place // bit) % 2))

    def at(bit):
        return {"fsdp": flipped(bit), "tp": side}

    def both(one, two):
        return {"fsdp": flipped(one) + flipped(two) - place, "tp": side}

    core, row, near_z, far_z = at(1), at(2), at(4), at(8)
    diagonal, third_z = both(4, 1), both(4, 8)
    twin = {"fsdp": place, "tp": 1 - side}
    z = place // 4
    is_inner = ((z + 1) // 2) % 2
    keep_late = (place // top + side) % 2

    pieces = piece_rows(half)
    columns = []
    low = 0
    for ref in (cq, ck, cv):
        columns.append((low, low + ref.shape[1]))
        low += ref.shape[1]

    def load_cot(i, m):
        low, high = columns[m]
        ref = (cq, ck, cv)[m]
        return pltpu.make_async_copy(
            ref.at[pl.ds(i * lanes, lanes), :],
            C.at[i, pl.ds(0, lanes), pl.ds(low, high - low)],
            load_c.at[i, m],
        )

    def load_weight(h, m):
        low, high = columns[m]
        ref = (wq, wk, wv)[m]
        return pltpu.make_async_copy(
            ref.at[pl.ds(h * half, half), :],
            W.at[h, :, pl.ds(low, high - low)],
            load_w.at[h, m],
        )

    def remote(src, dst, send, recv, device):
        return pltpu.make_async_remote_copy(
            src_ref=src, dst_ref=dst, send_sem=send, recv_sem=recv,
            device_id=device, device_id_type=pl.DeviceIdType.MESH,
        )

    lower, upper = pl.ds(0, lanes), pl.ds(lanes, lanes)
    full_width, owned, rank, scale = settings
    own_columns = pl.ds(pl.multiple_of(side * owned, lanes), owned)
    feature_blocks = owned // lanes
    share = F.shape[0] // 2
    core_index, row_index = place % 2, (place // 2) % 2
    part_start = core_index * share + row_index * (share // 2)
    piece = share // 8

    small_loads = [
        pltpu.make_async_copy(tokens, T, load_s.at[0]),
        pltpu.make_async_copy(gain.at[:, own_columns], GA, load_s.at[1]),
    ]
    for m in range(3):
        small_loads.append(
            pltpu.make_async_copy(
                adapters.at[m, :, own_columns], D.at[pl.ds(rank * m, rank)], load_s.at[2 + m]
            )
        )
        low, high = columns[m]
        small_loads.append(
            pltpu.make_async_copy(
                (uq, uk, uv)[m],
                U.at[pl.ds(rank * m, rank), pl.ds(low, high - low)],
                load_s.at[5 + m],
            )
        )

    def pair_rows():
        return remote(A, AR, a_send, a_recv, twin)

    def inner_rows(i):
        return remote(I.at[i], IR.at[i], i_send, i_recv.at[i], twin)

    def grads_core():
        away = (1 - core_index) * share
        return remote(G.at[pl.ds(away, share)], GC, gc_send, gc_recv, core)

    def grads_row():
        away = core_index * share + (1 - row_index) * (share // 2)
        return remote(G.at[pl.ds(away, share // 2)], GY, gy_send, gy_recv, row)

    z_partners = ((near_z, 1), (far_z, 2), (third_z, 3))

    def z_flip(bits):
        low, high = z % 2, z // 2
        low = 1 - low if bits % 2 else low
        high = 1 - high if bits // 2 else high
        return 2 * high + low

    def grads_z(n):
        device, bits = z_partners[n]
        return remote(
            H.at[pl.ds(z_flip(bits) * piece, piece)], HZ.at[n], gz_send, gz_recv.at[n], device
        )

    mine_z = pl.ds(part_start + z * piece, piece)
    mine_y = pl.ds(part_start, share // 2)
    mine_c = pl.ds(core_index * share, share)

    def spread_z(n):
        return remote(F.at[mine_z], F.at[mine_z], ga_send, ga_recv.at[n], z_partners[n][0])

    def spread_y():
        return remote(F.at[mine_y], F.at[mine_y], gb_send, gb_recv, row)

    def spread_c():
        return remote(F.at[mine_c], F.at[mine_c], gd_send, gd_recv, core)

    def cot_core(i):
        return remote(C.at[i, lower], C.at[i, upper], cc_send, cc_recv.at[i], core)

    def cot_z(i):
        return remote(C.at[i, lower], C.at[count + i, lower], cz_send, cz_recv.at[i], near_z)

    def cot_zc(i):
        return remote(
            C.at[count + i, lower], C.at[count + i, upper], zc_send, zc_recv.at[i], core
        )

    def weight_y(h):
        return remote(W.at[h], W.at[2 + h], y_send, y_recv.at[h], row)

    def far(h, k):
        low, high = pieces[k]
        rows = pl.ds(low, high - low)
        return remote(W.at[h, rows], W.at[4 + h, rows], far_send, far_recv.at[h, k], far_z)

    def far_y(h, k):
        low, high = pieces[k]
        rows = pl.ds(low, high - low)
        return remote(W.at[4 + h, rows], W.at[6 + h, rows], fy_send, fy_recv.at[h, k], row)

    for i in range(count):
        for m in range(3):
            load_cot(i, m).start()
    for h in range(2):
        for m in range(3):
            load_weight(h, m).start()
    for copy in small_loads:
        copy.start()

    barrier = pltpu.get_barrier_semaphore()
    partners = (core, row, near_z, diagonal, far_z, third_z, twin)
    for partner in partners:
        pl.semaphore_signal(
            barrier, inc=1, device_id=partner, device_id_type=pl.DeviceIdType.MESH
        )
    pl.semaphore_wait(barrier, len(partners))

    for i in range(count):
        for m in range(3):
            load_cot(i, m).wait()

        @pl.when(is_inner == 0)
        def _():
            cot_z(i).start()

    for h in range(2):
        for m in range(3):
            load_weight(h, m).wait()

        @pl.when(is_inner == 1)
        def _():
            for k in range(len(pieces)):
                far(h, k).start()

        if h == 0:
            weight_y(h).start()
    for i in range(count):
        cot_core(i).start()

    lane = lax.broadcasted_iota(jnp.int32, (lanes, lanes), 1)
    used = 3 * rank
    D[pl.ds(used, lanes - used), :] = jnp.zeros((lanes - used, owned), jnp.bfloat16)
    U[pl.ds(used, lanes - used), :] = jnp.zeros((lanes - used, U.shape[1]), jnp.bfloat16)
    for m in range(3):
        for other in range(3):
            if other != m:
                low, high = columns[other]
                U[pl.ds(rank * m, rank), pl.ds(low, high - low)] = jnp.zeros(
                    (rank, high - low), jnp.bfloat16
                )
    for p in range(3):
        GD[p] = jnp.zeros((lanes, owned), jnp.bfloat16)
    for copy in small_loads:
        copy.wait()
    rest = D[pl.ds(0, used), :].astype(jnp.float32) * GA[...]
    for p in range(3):
        part = rest.astype(jnp.bfloat16)
        GD[p, pl.ds(64, used), :] = part
        rest = rest - part.astype(jnp.float32)

    def nt_dot(left, right):
        return lax.dot_general(
            left, right, (((1,), (1,)), ((), ())), preferred_element_type=jnp.float32
        )

    for i in range(count):
        rows = pl.ds(i * lanes, lanes)
        own_rows = T[rows, :]
        value = nt_dot(C[i, lower, :], U[...])
        for p in range(3):
            value = value + nt_dot(own_rows, GD[p])
        wide = own_rows.astype(jnp.float32)
        squares = jnp.sum(wide * wide, axis=1, keepdims=True)
        A[i] = value + jnp.where(lane == 120, squares, 0.0)
    pair_rows().start()
    pair_rows().wait_recv()
    for i in range(count):
        rows = pl.ds(i * lanes, lanes)
        both_sum = A[i] + AR[i]
        squares = jnp.sum(jnp.where(lane == 120, both_sum, 0.0), axis=1, keepdims=True)
        inverse = lax.rsqrt(squares / full_width + norm_eps)
        INV[i] = jnp.broadcast_to(inverse, (lanes, lanes))
        low = jnp.where(lane < used, both_sum, 0.0)
        LO[i] = low.astype(jnp.bfloat16)
        scaled = jnp.where((lane >= 64) & (lane < 64 + used), both_sum * inverse, 0.0)
        ZT[:, rows] = (low + scaled).T.astype(jnp.bfloat16)
        N[rows, :] = (T[rows, :].astype(jnp.float32) * inverse * GA[...]).astype(jnp.bfloat16)

    def down_block(j, carry):
        cols = pl.ds(pl.multiple_of(j * lanes, lanes), lanes)
        value = scale * jnp.dot(
            ZT[pl.ds(0, 64), :], N[:, cols], preferred_element_type=jnp.float32
        )
        for m in range(3):
            G[m * feature_blocks + j] = value[rank * m : rank * (m + 1)]
        return carry

    lax.fori_loop(0, feature_blocks, down_block, 0)
    first = 3 * feature_blocks
    for m in range(3):
        low, high = columns[m]

        def up_block(j, carry, m=m, low=low):
            cols = pl.ds(pl.multiple_of(low + j * lanes, lanes), lanes)
            value = jnp.zeros((rank, lanes), jnp.float32)
            for i in range(count):
                value = value + jnp.dot(
                    ZT[pl.ds(64 + rank * m, rank), pl.ds(i * lanes, lanes)],
                    C[i, lower, cols],
                    preferred_element_type=jnp.float32,
                )
            G[first + low // lanes + j] = scale * value
            return carry

        lax.fori_loop(0, (high - low) // lanes, up_block, 0)
    filled = first + columns[2][1] // lanes
    for j in range(filled, G.shape[0]):
        G[j] = jnp.zeros((rank, lanes), jnp.float32)
    grads_core().start()
    grads_core().wait_recv()
    G[mine_c] = G[mine_c] + GC[...]
    grads_row().start()
    weight_y(1).start()

    (outer, outer_marks), (inner, inner_marks) = near_and_far_orders(count)
    tiles = len(outer)
    lag = 4

    def order_at(step):
        w = digit_at(step, is_inner, [a for a, _ in outer], [a for a, _ in inner])
        t = digit_at(step, is_inner, [b for _, b in outer], [b for _, b in inner])
        return w, t

    def when(step, outer_name, inner_name):
        o = outer_marks[outer_name] if outer_name else -1
        i = inner_marks[inner_name] if inner_name else -1
        return pl.when(step == is_inner * i + (1 - is_inner) * o)

    def take_far(h, k):
        far(h, k).wait_recv()
        far_y(h, k).start()

    def body(step, carry):
        @when(step, "near", "near")
        def _():
            for i in range(count):
                cot_core(i).wait_recv()

        @when(step, None, f"z{count - 1}")
        def _():
            remote(W.at[pl.ds(0, 2)], W.at[pl.ds(4, 2)], far_send, far_recv.at[0, 0], far_z).wait_send()
            for i in range(count - 1):
                cot_z(i).start()

        @when(step, "f0", "z1")
        def _():
            grads_row().wait_recv()
            G[mine_y] = G[mine_y] + GY[...]
            H[...] = G[mine_y].astype(jnp.bfloat16)
            for n in range(3):
                grads_z(n).start()

        @when(step, "y", None)
        def _():
            for k in range(len(pieces)):
                far(0, k).start()

        @when(step, "z0", "f0")
        def _():
            value = G[mine_z]
            for n in range(3):
                grads_z(n).wait_recv()
                value = value + HZ[n].astype(jnp.float32)
            F[mine_z] = value.astype(jnp.bfloat16)
            for n in range(3):
                spread_z(n).start()

        @when(step, "z0", None)
        def _():
            for k in range(len(pieces)):
                far(1, k).start()

        @when(step, None, "f0")
        def _():
            cot_z(count - 1).start()

        @when(step, "fy1", "f1")
        def _():
            for n in range(3):
                spread_z(n).wait_recv()
            spread_y().start()

        for i in range(count):
            @when(step, f"z{i}", f"z{i}")
            def _():
                cot_z(i).wait_recv()
                cot_zc(i).start()
                cot_zc(i).wait_recv()

        @when(step, "y", "y")
        def _():
            weight_y(0).wait_recv()
            weight_y(1).wait_recv()

        number = len(pieces)

        @when(step, "f0", "f0")
        def _():
            for k in range(number):
                take_far(0, k)

        split = number // 2

        @when(step, "f1", "fy0")
        def _():
            for k in range(split):
                take_far(1, k)

        @when(step, "f1", "f1")
        def _():
            for k in range(split, number):
                take_far(1, k)

        for h in range(2):
            @when(step, f"fy{h}", f"fy{h}")
            def _():
                for k in range(number):
                    far_y(h, k).wait_recv()

        w, t = order_at(step)

        @pl.when(step < tiles)
        def _():
            value = lax.dot_general(
                W[w], C[t], (((1,), (1,)), ((), ())), preferred_element_type=jnp.float32
            ).astype(jnp.bfloat16)
            S[w, t, 0] = value[:, :lanes]
            S[w, t, 1] = value[:, lanes:]

        @pl.when((step < tiles) & (w // 4 != keep_late))
        def _():
            remote(S.at[w, t], X.at[w % 4, t], x_send, x_recv.at[w % 4, t], twin).start()

        back = jnp.maximum(step - lag, 0)
        w2, t2 = order_at(back)

        @pl.when((step >= lag) & (w2 // 4 == keep_late))
        def _():
            remote(S.at[w2, t2], X.at[w2 % 4, t2], x_send, x_recv.at[w2 % 4, t2], twin).wait_recv()
            total = S[w2, t2].astype(jnp.float32) + X[w2 % 4, t2].astype(jnp.float32)
            S[w2, t2] = total.astype(jnp.bfloat16)
            base = place % top
            index = base + ((w2 // 2) % 2) * 2 * (1 - 2 * ((base // 2) % 2))
            rows = pl.ds(pl.multiple_of(index * block + (w2 % 2) * half, 16), half)
            i = t2 % count

            @pl.when(t2 < count)
            def _():
                R[i, rows, :] = total[0].astype(jnp.bfloat16)
                remote(S.at[w2, t2, 1], R.at[i, rows], r_send, r_recv, core).start()

            @pl.when(t2 >= count)
            def _():
                remote(S.at[w2, t2, 0], R.at[i, rows], r_send, r_recv, near_z).start()
                remote(S.at[w2, t2, 1], R.at[i, rows], r_send, r_recv, diagonal).start()

        return carry

    lax.fori_loop(0, tiles + lag, body, 0)

    spread_y().wait_recv()
    spread_c().start()
    part = pl.ds(0, 3 * R.shape[1] // 4)
    results = remote(R.at[:, part], R.at[:, part], r_send, r_recv, core)
    results.wait_recv()
    for i in range(count):
        rows = pl.ds(i * lanes, lanes)

        def gained_block(j, carry, i=i, rows=rows):
            cols = pl.ds(pl.multiple_of(j * lanes, lanes), lanes)
            back = R[i, cols, :].astype(jnp.float32).T
            back = back + adapter_scale * jnp.dot(
                LO[i], D[:, cols], preferred_element_type=jnp.float32
            )
            gained = GA[:, cols] * back
            B[rows, cols] = gained
            return carry + gained * (T[rows, cols].astype(jnp.float32) * INV[i])

        total = lax.fori_loop(0, feature_blocks, gained_block, jnp.zeros((lanes, lanes), jnp.float32))
        I[i] = jnp.broadcast_to(jnp.sum(total, axis=1, keepdims=True), (lanes, lanes))
        inner_rows(i).start()
    spread_c().wait_recv()
    for j in range(feature_blocks):
        for m in range(3):
            grad_down[m, :, pl.ds(j * lanes, lanes)] = F[m * feature_blocks + j].astype(jnp.float32)
    for m, ref in enumerate((grad_up_q, grad_up_k, grad_up_v)):
        low, high = columns[m]
        for j in range((high - low) // lanes):
            ref[:, pl.ds(j * lanes, lanes)] = F[first + low // lanes + j].astype(jnp.float32)
    for i in range(count):
        rows = pl.ds(i * lanes, lanes)
        inner_rows(i).wait_recv()
        inner = (I[i] + IR[i]) / full_width

        def final_block(j, carry, i=i, rows=rows, inner=inner):
            cols = pl.ds(pl.multiple_of(j * lanes, lanes), lanes)
            unit = T[rows, cols].astype(jnp.float32) * INV[i]
            out[rows, cols] = (INV[i] * (B[rows, cols] - unit * inner)).astype(jnp.bfloat16)
            return carry

        lax.fori_loop(0, feature_blocks, final_block, 0)

    results.wait_send()
    own = C.at[pl.ds(0, count), lower]
    remote(own, own, cc_send, cc_recv.at[0], core).wait_send()
    remote(own, own, cz_send, cz_recv.at[0], core).wait_send()
    remote(own, own, zc_send, zc_recv.at[0], core).wait_send()
    two = W.at[pl.ds(0, 2)]
    remote(two, two, y_send, y_recv.at[0], core).wait_send()

    @pl.when(is_inner == 0)
    def _():
        remote(two, two, far_send, far_recv.at[0, 0], core).wait_send()

    remote(two, two, fy_send, fy_recv.at[0, 0], core).wait_send()
    four = S.at[pl.ds(0, 4)]
    remote(four, four, x_send, x_recv.at[0, 0], core).wait_send()
    pair_rows().wait_send()
    remote(I, I, i_send, i_recv.at[0], twin).wait_send()
    grads_core().wait_send()
    grads_row().wait_send()
    three = H.at[pl.ds(0, 3 * piece)]
    remote(three, three, gz_send, gz_recv.at[0], core).wait_send()
    three = F.at[pl.ds(0, 3 * piece)]
    remote(three, three, ga_send, ga_recv.at[0], core).wait_send()
    spread_y().wait_send()
    spread_c().wait_send()


token_lanes = 128


def grid_fits(weights, cotangents, tokens, rank):
    rows = weights[0].shape[0]
    tokens_here, owned = tokens.shape
    count = tokens_here // token_lanes
    aligned = all(c.shape[1] % token_lanes == 0 for c in cotangents) and owned % token_lanes == 0
    return (
        aligned and rows % 32 == 0 and tokens_here % token_lanes == 0
        and count in (3, 4) and rank == 16 and owned == 8 * rows
    )


def grid_step(tokens, gain, weights, adapters, ups, cotangents):
    rows = weights[0].shape[0]
    tokens_here, owned = tokens.shape
    full_width = gain.shape[0]
    rank = adapters.shape[1]
    depth = sum(w.shape[1] for w in weights)
    half = rows // 2
    lanes = token_lanes
    count = tokens_here // lanes
    number = len(piece_rows(half))
    scale = adapter_scale / math.sqrt(tokens_here * lax.axis_size("fsdp"))
    grad_blocks = 16 * -(-(3 * owned + depth) // (16 * lanes))
    share = grad_blocks // 2
    DMA = pltpu.SemaphoreType.DMA
    f32, bf16 = jnp.float32, jnp.bfloat16
    vmem = pl.BlockSpec(memory_space=pltpu.VMEM)
    return pl.pallas_call(
        functools.partial(grid_kernel, (full_width, owned, rank, scale)),
        out_shape=(
            jax.ShapeDtypeStruct(tokens.shape, bf16),
            jax.ShapeDtypeStruct((3, rank, owned), f32),
        ) + tuple(jax.ShapeDtypeStruct((rank, c.shape[1]), f32) for c in cotangents),
        in_specs=[pl.BlockSpec(memory_space=pl.ANY)] * 12,
        out_specs=(vmem,) * 5,
        scratch_shapes=[
            pltpu.VMEM((8, half, depth), bf16),
            pltpu.VMEM((2 * count, 2 * lanes, depth), bf16),
            pltpu.VMEM((8, 2 * count, 2, half, lanes), bf16),
            pltpu.VMEM((4, 2 * count, 2, half, lanes), bf16),
            pltpu.VMEM((count, 8 * rows, lanes), bf16),
            pltpu.VMEM((tokens_here, owned), bf16),
            pltpu.VMEM((1, owned), f32),
            pltpu.VMEM((lanes, depth), bf16),
            pltpu.VMEM((lanes, owned), bf16),
            pltpu.VMEM((3, lanes, owned), bf16),
            pltpu.VMEM((count, lanes, lanes), f32),
            pltpu.VMEM((count, lanes, lanes), f32),
            pltpu.VMEM((count, lanes, lanes), f32),
            pltpu.VMEM((count, lanes, lanes), bf16),
            pltpu.VMEM((lanes, tokens_here), bf16),
            pltpu.VMEM((tokens_here, owned), bf16),
            pltpu.VMEM((tokens_here, owned), f32),
            pltpu.VMEM((count, lanes, lanes), f32),
            pltpu.VMEM((count, lanes, lanes), f32),
            pltpu.VMEM((grad_blocks, rank, lanes), f32),
            pltpu.VMEM((share, rank, lanes), f32),
            pltpu.VMEM((share // 2, rank, lanes), f32),
            pltpu.VMEM((share // 2, rank, lanes), bf16),
            pltpu.VMEM((3, share // 8, rank, lanes), bf16),
            pltpu.VMEM((grad_blocks, rank, lanes), bf16),
            DMA((2, 3)), DMA((count, 3)), DMA((8,)),
            DMA, DMA, DMA, DMA((count,)),
            DMA, DMA, DMA, DMA, DMA, DMA((3,)), DMA, DMA((3,)), DMA, DMA, DMA, DMA,
            DMA, DMA((count,)), DMA, DMA((count,)), DMA, DMA((count,)),
            DMA, DMA((2,)), DMA, DMA((2, number)), DMA, DMA((2, number)),
            DMA, DMA((4, 2 * count)), DMA, DMA,
        ],
        compiler_params=pltpu.CompilerParams(
            collective_id=0, has_side_effects=True, vmem_limit_bytes=60 * 1024 * 1024
        ),
        cost_estimate=pl.CostEstimate(
            flops=2 * 16 * rows * tokens_here * depth, bytes_accessed=2 * 8 * rows * depth,
            transcendentals=0,
        ),
        name="grid",
    )(*cotangents, *weights, tokens, gain.reshape(1, full_width), adapters, *ups)


def shards(
    tokens,
    gain,
    query_projection_weight,
    key_projection_weight,
    value_projection_weight,
    adapter_down_factors,
    query_adapter_up,
    key_adapter_up,
    value_adapter_up,
    query_cotangent,
    key_cotangent,
    value_cotangent,
):
    return device_work(
        tokens,
        gain,
        (query_projection_weight, key_projection_weight, value_projection_weight),
        adapter_down_factors,
        (query_adapter_up, key_adapter_up, value_adapter_up),
        (query_cotangent, key_cotangent, value_cotangent),
    )


def device_work(tokens, gain, weights, adapter_down_factors, ups, cots):
    fsdp_size = lax.axis_size("fsdp")
    tp_size = lax.axis_size("tp")
    tp_index = lax.axis_index("tp")
    row_count, owned = tokens.shape
    full_width = gain.shape[0]
    rank = adapter_down_factors.shape[1]
    if tp_size == 2 and fsdp_size == 16 and grid_fits(weights, cots, tokens, rank):
        return grid_step(tokens, gain, weights, adapter_down_factors, ups, cots)

    def tp_sum(value):
        if tp_size != 2:
            return lax.psum(value, "tp")
        with jax.named_scope("pair_sum"):
            return value + lax.ppermute(value, "tp", [(0, 1), (1, 0)])

    wide = tokens.astype(jnp.float32)
    gain_own = lax.dynamic_slice_in_dim(gain, tp_index * owned, owned, 0)
    down = lax.dynamic_slice_in_dim(adapter_down_factors, tp_index * owned, owned, 2)
    down = down.reshape(3 * rank, owned)
    low_in = lax.dot_general(
        wide * gain_own[None, :],
        down.astype(jnp.float32),
        (((1,), (1,)), ((), ())),
        precision=lax.Precision.HIGHEST,
    )
    low_out = jnp.concatenate([transposed_product(c, u) for c, u in zip(cots, ups)], axis=1)
    squares = jnp.sum(wide * wide, axis=1, keepdims=True)
    small = tp_sum(jnp.concatenate([squares, low_in, low_out], axis=1))
    inverse = lax.rsqrt(small[:, :1] / full_width + norm_eps)
    in_low = (small[:, 1 : 1 + 3 * rank] * inverse).astype(jnp.bfloat16)
    out_low = small[:, 1 + 3 * rank :].astype(jnp.bfloat16)
    unit_rows = wide * inverse
    normed = (unit_rows * gain_own[None, :]).astype(jnp.bfloat16)
    scale = adapter_scale / math.sqrt(row_count * fsdp_size)

    def token_product(left, right):
        return scale * lax.dot_general(
            left, right, (((0,), (0,)), ((), ())), preferred_element_type=jnp.float32
        )

    down_local = token_product(out_low, normed)
    up_local = [
        token_product(in_low[:, rank * m : rank * (m + 1)], cots[m]) for m in range(3)
    ]
    small_work = tuple(down_local[rank * m : rank * (m + 1)] for m in range(3)) + tuple(up_local)
    back = plain_back(weights, cots, full_width)
    grads = lax.psum(jnp.concatenate(small_work, axis=1), "fsdp")
    grad_down = jnp.stack([grads[:, owned * m : owned * (m + 1)] for m in range(3)])
    ends = [3 * owned]
    for cot in cots:
        ends.append(ends[-1] + cot.shape[1])
    up_q, up_k, up_v = [grads[:, low:high] for low, high in zip(ends[:-1], ends[1:])]

    back = back + adapter_scale * jnp.dot(out_low, down, preferred_element_type=jnp.float32)
    gained = gain_own[None, :] * back
    inner = tp_sum(jnp.sum(gained * unit_rows, axis=1, keepdims=True)) / full_width
    grad_tokens = (inverse * (gained - unit_rows * inner)).astype(jnp.bfloat16)
    return (grad_tokens, grad_down, up_q, up_k, up_v)


def solution(mesh):
    in_specs = (
        P("fsdp", "tp"),
        P(),
        P("fsdp", "tp"),
        P("fsdp", "tp"),
        P("fsdp", "tp"),
        P(),
        P(None, "tp"),
        P(None, "tp"),
        P(None, "tp"),
        P("fsdp", "tp"),
        P("fsdp", "tp"),
        P("fsdp", "tp"),
    )
    out_specs = (P("fsdp", "tp"), P(None, None, "tp"), P(None, "tp"), P(None, "tp"), P(None, "tp"))
    step = jax.shard_map(shards, mesh=mesh, in_specs=in_specs, out_specs=out_specs, check_vma=False)
    return step
```

profile of v0, /device:TPU:0, one launch (start us, length us, event | category | flops | bytes accessed | tf_op | source)
XLA Modules:
  0.0 204.7 jit_solution(1482053463998453788)
XLA Ops:
  0.6 1.4 reshape.13.gain
  2.0 196.7 %grid.1 = (bf16[384,2816]{1,0:T(8,128)(2,1)}, f32[3,16,2816]{2,1,0:T(8,128)}, f32[16,3072]{1,0:T(8,128)}, f32[16,512]{1,0:T(8,128)}, f32[16,512]{1,0:T(8,128)}) custom-call(bf16[384,3072]{1,0:T(8,128)(2,1)} %cq.1, bf16[384,512]{1,0:T(8,128)(2,1)} %ck.1, bf16[384,512]{1,0:T(8,128)(2,1)} %cv.1, bf16[352,3072]{1,0:T(8,128)(2,1)} %wq.1, bf16[352,512]{1,0:T(8,128)(2,1)} %wk.1, ...), custom_call_target="tpu_custom_call" | custom-call | flops 17716740096 | bytes 23068672 | tf_op jit(solution)/shard_map/grid/pallas_call | solution.py:616
  198.7 0.0 copy-start
  198.8 0.0 copy-start.1
  198.8 0.0 copy-start.3
  198.8 0.0 copy-start.2
  198.8 3.2 %copy.22 = bf16[384,2816]{1,0:T(8,128)(2,1)} copy(bf16[384,2816]{1,0:T(8,128)(2,1)} %get-tuple-element.10) | data formatting | bytes 4325376
  201.9 0.0 copy-done
  201.9 0.8 copy.23
  202.7 0.0 copy-done.1
  202.7 0.7 copy.24
  203.4 0.0 copy-done.3
  203.4 0.6 copy.25
  204.0 0.0 copy-done.2
  204.0 0.6 copy.26
Async XLA Ops:
  198.7 3.2 %copy-start = (f32[3,16,2816]{2,1,0:T(8,128)S(1)}, f32[3,16,2816]{2,1,0:T(8,128)}, u32[]{:S(2)}) copy-start(f32[3,16,2816]{2,1,0:T(8,128)} %get-tuple-element.11) | copy-start | bytes 1622020
  198.8 4.0 %copy-start.1 = (f32[16,3072]{1,0:T(8,128)S(1)}, f32[16,3072]{1,0:T(8,128)}, u32[]{:S(2)}) copy-start(f32[16,3072]{1,0:T(8,128)} %get-tuple-element.12) | copy-start | bytes 589828
  198.8 4.7 %copy-start.3 = (f32[16,512]{1,0:T(8,128)S(1)}, f32[16,512]{1,0:T(8,128)}, u32[]{:S(2)}) copy-start(f32[16,512]{1,0:T(8,128)} %get-tuple-element.13) | copy-start | bytes 98308
  198.8 5.3 %copy-start.2 = (f32[16,512]{1,0:T(8,128)S(1)}, f32[16,512]{1,0:T(8,128)}, u32[]{:S(2)}) copy-start(f32[16,512]{1,0:T(8,128)} %get-tuple-element.14) | copy-start | bytes 98308
where the time goes:
time: 205 us
  Pallas kernels  197 us (96%)
  local copies, waits for them, and re-layouts  7.24 us (4%)
    pallas_call x1, Pallas kernels, grid_step(): pl.pallas_call(functools.partial(grid_kernel, (full_width, owned, rank, s...  197 us
    unnamed x13, local copies, waits for them, and re-layouts  5.87 us

commit v1 on v0

--- a/solution.py
+++ b/solution.py
@@ -27,38 +27,43 @@
 
 
 def near_and_far_orders(count):
-    near = range(count)
+    near = list(range(count))
+    every = list(range(2 * count))
     outer, outer_marks = [], {}
     inner, inner_marks = [], {}
 
-    def add(order, marks, name, tiles):
+    def add(order, marks, name, groups, ts):
         marks[name] = len(order)
-        order.extend(tiles)
-
-    def grid(ws, ts):
-        return [(w, t) for w in ws for t in ts]
-
-    add(outer, outer_marks, "near", grid((0, 1), near))
-    add(outer, outer_marks, "f0", grid((4,), near))
-    add(outer, outer_marks, "y", grid((2, 3), near))
-    add(outer, outer_marks, "f1", grid((5,), near))
-    done = [0, 1, 2, 3, 4, 5]
+        order.extend((w, t, n) for t in ts for w, n in groups)
+
+    own, row = (0, 2), (2, 2)
+    first, second = (4, 2), (6, 2)
+    add(outer, outer_marks, "near", [own], near)
+    add(outer, outer_marks, "f0", [(4, 1)], near)
+    add(outer, outer_marks, "y", [row], near)
+    add(outer, outer_marks, "f1", [(6, 1)], near)
+    late = [(4, 1), (6, 1)]
     for i in range(count):
-        add(outer, outer_marks, f"z{i}", grid(done, (count + i,)))
-        if i >= count - 3 and i < count - 1:
-            w = 6 + i - (count - 3)
-            add(outer, outer_marks, f"fy{w - 6}", grid((w,), range(count + i + 1)))
-            done.append(w)
-    every = range(2 * count)
-    add(inner, inner_marks, "near", grid((0, 1), near))
+        add(outer, outer_marks, f"z{i}", [own, row] + late, [count + i])
+        if i == count - 3:
+            add(outer, outer_marks, "fy0", [(5, 1)], range(count + i + 1))
+            late = [first, (6, 1)]
+        if i == count - 2:
+            add(outer, outer_marks, "fy1", [(7, 1)], range(count + i + 1))
+            late = [first, second]
+    add(inner, inner_marks, "near", [own], near)
     for i in range(count):
-        add(inner, inner_marks, f"z{i}", grid((0, 1), (count + i,)))
-    add(inner, inner_marks, "y", grid((2, 3), every))
-    add(inner, inner_marks, "f0", grid((4,), every))
-    add(inner, inner_marks, "fy0", grid((6,), every))
-    add(inner, inner_marks, "f1", grid((5,), every))
-    add(inner, inner_marks, "fy1", grid((7,), every))
-    return (outer, outer_marks), (inner, inner_marks)
+        add(inner, inner_marks, f"z{i}", [own], [count + i])
+    add(inner, inner_marks, "y", [row], every)
+    add(inner, inner_marks, "f0", [(4, 1)], every)
+    add(inner, inner_marks, "fy0", [(5, 1)], every)
+    add(inner, inner_marks, "f1", [(6, 1)], every)
+    add(inner, inner_marks, "fy1", [(7, 1)], every)
+    steps = max(len(outer), len(inner))
+    lengths = len(outer), len(inner)
+    for order in (outer, inner):
+        order.extend([(0, 0, 0)] * (steps - len(order)))
+    return (outer, outer_marks), (inner, inner_marks), lengths
 
 
 def packed(digits):
@@ -85,11 +90,11 @@
 def grid_kernel(
     settings,
     cq, ck, cv, wq, wk, wv, tokens, gain, adapters, uq, uk, uv,
-    out, grad_down, grad_up_q, grad_up_k, grad_up_v,
+    out, inner_out, inverse_out, grad_down, grad_up_q, grad_up_k, grad_up_v,
     W, C, S, X, R,
-    T, GA, U, D, GD, A, AR, INV, LO, ZT, N, B, I, IR,
+    T, GW, GA, U, D, GD, A, AR, INV, LO, ZT, N, B, I, IR,
     G, GC, GY, H, HZ, F,
-    load_w, load_c, load_s,
+    load_w, load_c, load_s, store_sem,
     a_send, a_recv, i_send, i_recv,
     gc_send, gc_recv, gy_send, gy_recv, gz_send, gz_recv, ga_send, ga_recv, gb_send, gb_recv, gd_send, gd_recv,
     cc_send, cc_recv, cz_send, cz_recv, zc_send, zc_recv,
@@ -162,7 +167,7 @@
 
     small_loads = [
         pltpu.make_async_copy(tokens, T, load_s.at[0]),
-        pltpu.make_async_copy(gain.at[:, own_columns], GA, load_s.at[1]),
+        pltpu.make_async_copy(gain, GW, load_s.at[1]),
     ]
     for m in range(3):
         small_loads.append(
@@ -226,6 +231,15 @@
     def cot_z(i):
         return remote(C.at[i, lower], C.at[count + i, lower], cz_send, cz_recv.at[i], near_z)
 
+    cot_pieces = [(i, low) for i in range(count) for low in range(0, lanes, 32)]
+
+    def start_cot_pieces(low, high):
+        for i, first in cot_pieces[low:high]:
+            rows = pl.ds(first, 32)
+            remote(
+                C.at[i, rows], C.at[count + i, rows], cz_send, cz_recv.at[i], near_z
+            ).start()
+
     def cot_zc(i):
         return remote(
             C.at[count + i, lower], C.at[count + i, upper], zc_send, zc_recv.at[i], core
@@ -237,12 +251,12 @@
     def far(h, k):
         low, high = pieces[k]
         rows = pl.ds(low, high - low)
-        return remote(W.at[h, rows], W.at[4 + h, rows], far_send, far_recv.at[h, k], far_z)
+        return remote(W.at[h, rows], W.at[4 + 2 * h, rows], far_send, far_recv.at[h, k], far_z)
 
     def far_y(h, k):
         low, high = pieces[k]
         rows = pl.ds(low, high - low)
-        return remote(W.at[4 + h, rows], W.at[6 + h, rows], fy_send, fy_recv.at[h, k], row)
+        return remote(W.at[4 + 2 * h, rows], W.at[5 + 2 * h, rows], fy_send, fy_recv.at[h, k], row)
 
     for i in range(count):
         for m in range(3):
@@ -298,6 +312,8 @@
         GD[p] = jnp.zeros((lanes, owned), jnp.bfloat16)
     for copy in small_loads:
         copy.wait()
+    for j in range(feature_blocks):
+        GA[:, pl.ds(j * lanes, lanes)] = GW[pl.ds(side * feature_blocks + j, 1), :]
     rest = D[pl.ds(0, used), :].astype(jnp.float32) * GA[...]
     for p in range(3):
         part = rest.astype(jnp.bfloat16)
@@ -368,24 +384,46 @@
     grads_row().start()
     weight_y(1).start()
 
-    (outer, outer_marks), (inner, inner_marks) = near_and_far_orders(count)
-    tiles = len(outer)
-    lag = 4
+    (outer, outer_marks), (inner, inner_marks), lengths = near_and_far_orders(count)
+    tiles = is_inner * lengths[1] + (1 - is_inner) * lengths[0]
+    lag = 3
 
     def order_at(step):
-        w = digit_at(step, is_inner, [a for a, _ in outer], [a for a, _ in inner])
-        t = digit_at(step, is_inner, [b for _, b in outer], [b for _, b in inner])
-        return w, t
-
-    def when(step, outer_name, inner_name):
+        return [
+            digit_at(step, is_inner, [a[k] for a in outer], [a[k] for a in inner])
+            for k in range(3)
+        ]
+
+    def when(step, outer_name, inner_name, inner_shift=0):
         o = outer_marks[outer_name] if outer_name else -1
-        i = inner_marks[inner_name] if inner_name else -1
+        i = inner_marks[inner_name] + inner_shift if inner_name else -1
         return pl.when(step == is_inner * i + (1 - is_inner) * o)
 
     def take_far(h, k):
         far(h, k).wait_recv()
         far_y(h, k).start()
 
+    last_outer = f"z{count - 1}"
+    last_step = is_inner * inner_marks["f1"] + (1 - is_inner) * outer_marks[last_outer]
+    waiting = is_inner * count + (1 - is_inner) * (count - 1)
+
+    def sum_rows(slot):
+        base = place % top
+        other = keep_late * (slot % 2) + (1 - keep_late) * (slot // 2)
+        part = keep_late * (slot // 2) + (1 - keep_late) * (slot % 2)
+        index = base + other * 2 * (1 - 2 * ((base // 2) % 2))
+        return pl.ds(pl.multiple_of(index * block + part * half, 16), half)
+
+    def return_far(mine, t2, rows):
+        i = t2 - count
+        remote(S.at[mine, t2, 0], R.at[i, rows], r_send, r_recv.at[i], near_z).start()
+        remote(S.at[mine, t2, 1], R.at[i, rows], r_send, r_recv.at[i], diagonal).start()
+
+    def return_held(n, carry):
+        slot, i = n % 4, n // 4
+        return_far(slot, count + i, sum_rows(slot))
+        return carry
+
     def body(step, carry):
         @when(step, "near", "near")
         def _():
@@ -395,8 +433,7 @@
         @when(step, None, f"z{count - 1}")
         def _():
             remote(W.at[pl.ds(0, 2)], W.at[pl.ds(4, 2)], far_send, far_recv.at[0, 0], far_z).wait_send()
-            for i in range(count - 1):
-                cot_z(i).start()
+            start_cot_pieces(0, 4)
 
         @when(step, "f0", "z1")
         def _():
@@ -426,11 +463,7 @@
             for k in range(len(pieces)):
                 far(1, k).start()
 
-        @when(step, None, "f0")
-        def _():
-            cot_z(count - 1).start()
-
-        @when(step, "fy1", "f1")
+        @when(step, last_outer, "fy1")
         def _():
             for n in range(3):
                 spread_z(n).wait_recv()
@@ -450,22 +483,30 @@
 
         number = len(pieces)
 
-        @when(step, "f0", "f0")
+        @when(step, "f0", None)
         def _():
             for k in range(number):
                 take_far(0, k)
 
-        split = number // 2
-
-        @when(step, "f1", "fy0")
-        def _():
-            for k in range(split):
+        @when(step, "f1", None)
+        def _():
+            for k in range(number):
                 take_far(1, k)
 
-        @when(step, "f1", "f1")
-        def _():
-            for k in range(split, number):
-                take_far(1, k)
+        @pl.when((step == last_step) & (keep_late == 0))
+        def _():
+            lax.fori_loop(0, 4 * waiting, return_held, 0)
+
+        waves = number // 2
+        extra = -(-(len(cot_pieces) - 4) // number)
+        takes = [("f0", (k - number + 2) * 3 if k < number - 2 else 0) for k in range(number)]
+        takes += [("fy0", 0)] * waves + [("f1", 0)] * (number - waves)
+        for k, (name, shift) in enumerate(takes):
+            @when(step, None, name, shift)
+            def _():
+                take_far(k // number, k % number)
+                if k < number:
+                    start_cot_pieces(4 + extra * k, 4 + extra * (k + 1))
 
         for h in range(2):
             @when(step, f"fy{h}", f"fy{h}")
@@ -473,68 +514,66 @@
                 for k in range(number):
                     far_y(h, k).wait_recv()
 
-        w, t = order_at(step)
-
-        @pl.when(step < tiles)
-        def _():
+        w, t, n = order_at(step)
+
+        def product(size):
             value = lax.dot_general(
-                W[w], C[t], (((1,), (1,)), ((), ())), preferred_element_type=jnp.float32
+                W[pl.ds(w, size)].reshape(size * half, W.shape[2]),
+                C[t],
+                (((1,), (1,)), ((), ())),
+                preferred_element_type=jnp.float32,
             ).astype(jnp.bfloat16)
-            S[w, t, 0] = value[:, :lanes]
-            S[w, t, 1] = value[:, lanes:]
-
-        @pl.when((step < tiles) & (w // 4 != keep_late))
-        def _():
-            remote(S.at[w, t], X.at[w % 4, t], x_send, x_recv.at[w % 4, t], twin).start()
+            for q in range(size):
+                for part in range(2):
+                    S[w + q, t, part] = value[
+                        half * q : half * (q + 1), lanes * part : lanes * (part + 1)
+                    ]
+
+        @pl.when((step < tiles) & (n == 1))
+        def _():
+            product(1)
+
+        @pl.when((step < tiles) & (n == 2))
+        def _():
+            product(2)
+
+        for q in range(2):
+            @pl.when((step < tiles) & (q < n) & (w // 4 != keep_late))
+            def _():
+                remote(
+                    S.at[w + q, t], X.at[w % 4 + q, t], x_send, x_recv.at[w % 4 + q, t], twin
+                ).start()
 
         back = jnp.maximum(step - lag, 0)
-        w2, t2 = order_at(back)
-
-        @pl.when((step >= lag) & (w2 // 4 == keep_late))
-        def _():
-            remote(S.at[w2, t2], X.at[w2 % 4, t2], x_send, x_recv.at[w2 % 4, t2], twin).wait_recv()
-            total = S[w2, t2].astype(jnp.float32) + X[w2 % 4, t2].astype(jnp.float32)
-            S[w2, t2] = total.astype(jnp.bfloat16)
-            base = place % top
-            index = base + ((w2 // 2) % 2) * 2 * (1 - 2 * ((base // 2) % 2))
-            rows = pl.ds(pl.multiple_of(index * block + (w2 % 2) * half, 16), half)
-            i = t2 % count
-
-            @pl.when(t2 < count)
+        w2, t2, n2 = order_at(back)
+
+        for q in range(2):
+            @pl.when((step >= lag) & (step < tiles + lag) & (q < n2) & (w2 // 4 == keep_late))
             def _():
-                R[i, rows, :] = total[0].astype(jnp.bfloat16)
-                remote(S.at[w2, t2, 1], R.at[i, rows], r_send, r_recv, core).start()
-
-            @pl.when(t2 >= count)
-            def _():
-                remote(S.at[w2, t2, 0], R.at[i, rows], r_send, r_recv, near_z).start()
-                remote(S.at[w2, t2, 1], R.at[i, rows], r_send, r_recv, diagonal).start()
+                mine, slot = w2 + q, w2 % 4 + q
+                remote(
+                    S.at[mine, t2], X.at[slot, t2], x_send, x_recv.at[slot, t2], twin
+                ).wait_recv()
+                total = S[mine, t2].astype(jnp.float32) + X[slot, t2].astype(jnp.float32)
+                S[mine, t2] = total.astype(jnp.bfloat16)
+                rows = sum_rows(slot)
+                i = t2 % count
+
+                @pl.when(t2 < count)
+                def _():
+                    R[i, rows, :] = total[0].astype(jnp.bfloat16)
+                    remote(S.at[mine, t2, 1], R.at[i, rows], r_send, r_recv.at[i], core).start()
+
+                @pl.when((t2 >= count) & ((keep_late == 1) | (t2 >= count + waiting)))
+                def _():
+                    return_far(mine, t2, rows)
 
         return carry
 
-    lax.fori_loop(0, tiles + lag, body, 0)
+    lax.fori_loop(0, max(lengths) + lag, body, 0)
 
     spread_y().wait_recv()
     spread_c().start()
-    part = pl.ds(0, 3 * R.shape[1] // 4)
-    results = remote(R.at[:, part], R.at[:, part], r_send, r_recv, core)
-    results.wait_recv()
-    for i in range(count):
-        rows = pl.ds(i * lanes, lanes)
-
-        def gained_block(j, carry, i=i, rows=rows):
-            cols = pl.ds(pl.multiple_of(j * lanes, lanes), lanes)
-            back = R[i, cols, :].astype(jnp.float32).T
-            back = back + adapter_scale * jnp.dot(
-                LO[i], D[:, cols], preferred_element_type=jnp.float32
-            )
-            gained = GA[:, cols] * back
-            B[rows, cols] = gained
-            return carry + gained * (T[rows, cols].astype(jnp.float32) * INV[i])
-
-        total = lax.fori_loop(0, feature_blocks, gained_block, jnp.zeros((lanes, lanes), jnp.float32))
-        I[i] = jnp.broadcast_to(jnp.sum(total, axis=1, keepdims=True), (lanes, lanes))
-        inner_rows(i).start()
     spread_c().wait_recv()
     for j in range(feature_blocks):
         for m in range(3):
@@ -543,19 +582,37 @@
         low, high = columns[m]
         for j in range((high - low) // lanes):
             ref[:, pl.ds(j * lanes, lanes)] = F[first + low // lanes + j].astype(jnp.float32)
+    part = pl.ds(0, 3 * R.shape[1] // 4)
+    stores = []
+    for i in range(count):
+        rows = pl.ds(i * lanes, lanes)
+        remote(R.at[i, part], R.at[i, part], r_send, r_recv.at[i], core).wait_recv()
+        inverse = INV[i]
+
+        def gained_block(j, carry, i=i, rows=rows, inverse=inverse):
+            cols = pl.ds(pl.multiple_of(j * lanes, lanes), lanes)
+            back = R[i, cols, :].astype(jnp.float32).T
+            back = back + adapter_scale * jnp.dot(
+                LO[i], D[:, cols], preferred_element_type=jnp.float32
+            )
+            gained = GA[:, cols] * back
+            B[rows, cols] = gained
+            return carry + gained * (T[rows, cols].astype(jnp.float32) * inverse)
+
+        total = lax.fori_loop(
+            0, feature_blocks, gained_block, jnp.zeros((lanes, lanes), jnp.float32), unroll=2
+        )
+        I[i] = jnp.broadcast_to(jnp.sum(total, axis=1, keepdims=True), (lanes, lanes))
+        inner_rows(i).start()
+        stores.append(pltpu.make_async_copy(B.at[rows], out.at[rows], store_sem.at[i]))
+        stores[-1].start()
     for i in range(count):
         rows = pl.ds(i * lanes, lanes)
         inner_rows(i).wait_recv()
-        inner = (I[i] + IR[i]) / full_width
-
-        def final_block(j, carry, i=i, rows=rows, inner=inner):
-            cols = pl.ds(pl.multiple_of(j * lanes, lanes), lanes)
-            unit = T[rows, cols].astype(jnp.float32) * INV[i]
-            out[rows, cols] = (INV[i] * (B[rows, cols] - unit * inner)).astype(jnp.bfloat16)
-            return carry
-
-        lax.fori_loop(0, feature_blocks, final_block, 0)
-
+        inner_out[rows, :] = (I[i] + IR[i]) / full_width
+        inverse_out[rows, :] = INV[i]
+
+    results = remote(R.at[:, part], R.at[:, part], r_send, r_recv.at[0], core)
     results.wait_send()
     own = C.at[pl.ds(0, count), lower]
     remote(own, own, cc_send, cc_recv.at[0], core).wait_send()
@@ -581,9 +638,24 @@
     remote(three, three, ga_send, ga_recv.at[0], core).wait_send()
     spread_y().wait_send()
     spread_c().wait_send()
+    for store in stores:
+        store.wait()
 
 
 token_lanes = 128
+
+
+def final_kernel(gained, tokens, inner, inverse, *refs):
+    grads, (out, *grad_outs) = refs[:4], refs[4:]
+
+    @pl.when(pl.program_id(0) == 0)
+    def _():
+        for source, target in zip(grads, grad_outs):
+            target[...] = source[...]
+
+    scale = inverse[:, :1]
+    unit = tokens[...].astype(jnp.float32) * scale
+    out[...] = (scale * (gained[...] - unit * inner[:, :1])).astype(out.dtype)
 
 
 def grid_fits(weights, cotangents, tokens, rank):
@@ -613,14 +685,16 @@
     DMA = pltpu.SemaphoreType.DMA
     f32, bf16 = jnp.float32, jnp.bfloat16
     vmem = pl.BlockSpec(memory_space=pltpu.VMEM)
-    return pl.pallas_call(
+    gained, inner, inverse, *grads = pl.pallas_call(
         functools.partial(grid_kernel, (full_width, owned, rank, scale)),
         out_shape=(
-            jax.ShapeDtypeStruct(tokens.shape, bf16),
+            jax.ShapeDtypeStruct(tokens.shape, f32),
+            jax.ShapeDtypeStruct((tokens_here, lanes), f32),
+            jax.ShapeDtypeStruct((tokens_here, lanes), f32),
             jax.ShapeDtypeStruct((3, rank, owned), f32),
         ) + tuple(jax.ShapeDtypeStruct((rank, c.shape[1]), f32) for c in cotangents),
         in_specs=[pl.BlockSpec(memory_space=pl.ANY)] * 12,
-        out_specs=(vmem,) * 5,
+        out_specs=(pl.BlockSpec(memory_space=pl.ANY),) + (vmem,) * 6,
         scratch_shapes=[
             pltpu.VMEM((8, half, depth), bf16),
             pltpu.VMEM((2 * count, 2 * lanes, depth), bf16),
@@ -628,6 +702,7 @@
             pltpu.VMEM((4, 2 * count, 2, half, lanes), bf16),
             pltpu.VMEM((count, 8 * rows, lanes), bf16),
             pltpu.VMEM((tokens_here, owned), bf16),
+            pltpu.VMEM((full_width // lanes, lanes), f32),
             pltpu.VMEM((1, owned), f32),
             pltpu.VMEM((lanes, depth), bf16),
             pltpu.VMEM((lanes, owned), bf16),
@@ -647,12 +722,12 @@
             pltpu.VMEM((share // 2, rank, lanes), bf16),
             pltpu.VMEM((3, share // 8, rank, lanes), bf16),
             pltpu.VMEM((grad_blocks, rank, lanes), bf16),
-            DMA((2, 3)), DMA((count, 3)), DMA((8,)),
+            DMA((2, 3)), DMA((count, 3)), DMA((8,)), DMA((count,)),
             DMA, DMA, DMA, DMA((count,)),
             DMA, DMA, DMA, DMA, DMA, DMA((3,)), DMA, DMA((3,)), DMA, DMA, DMA, DMA,
             DMA, DMA((count,)), DMA, DMA((count,)), DMA, DMA((count,)),
             DMA, DMA((2,)), DMA, DMA((2, number)), DMA, DMA((2, number)),
-            DMA, DMA((4, 2 * count)), DMA, DMA,
+            DMA, DMA((4, 2 * count)), DMA, DMA((count,)),
         ],
         compiler_params=pltpu.CompilerParams(
             collective_id=0, has_side_effects=True, vmem_limit_bytes=60 * 1024 * 1024
@@ -662,7 +737,25 @@
             transcendentals=0,
         ),
         name="grid",
-    )(*cotangents, *weights, tokens, gain.reshape(1, full_width), adapters, *ups)
+    )(*cotangents, *weights, tokens, gain.reshape(full_width // lanes, lanes), adapters, *ups)
+    step_rows = 64
+
+    def by_rows(width):
+        return pl.BlockSpec((step_rows, width), lambda i: (i, 0))
+
+    whole = [pl.BlockSpec(g.shape, lambda i, k=len(g.shape): (0,) * k) for g in grads]
+    return pl.pallas_call(
+        final_kernel,
+        grid=(tokens_here // step_rows,),
+        out_shape=(jax.ShapeDtypeStruct(tokens.shape, bf16),)
+        + tuple(jax.ShapeDtypeStruct(g.shape, f32) for g in grads),
+        in_specs=[by_rows(owned), by_rows(owned), by_rows(lanes), by_rows(lanes), *whole],
+        out_specs=(by_rows(owned), *whole),
+        cost_estimate=pl.CostEstimate(
+            flops=4 * tokens_here * owned, bytes_accessed=8 * tokens_here * owned, transcendentals=0
+        ),
+        name="final",
+    )(gained, tokens, inner, inverse, *grads)
 
 
 def shards(

time: 205 us -> 186 us (0.907)
  Pallas kernels: 197 us -> 185 us
  local copies, waits for them, and re-layouts: 7.24 us -> 0 us
    pallas_call x1, Pallas kernels: 197 us -> 178 us  [grid_step(): pl.pallas_call(functools.partial(grid_kernel, (full_width, owned, rank, s...]
    pallas_call x0 -> x1, Pallas kernels: none -> 6.64 us  [grid_step(): pl.pallas_call(final_kernel, grid=(tokens_here // step_rows,), out_shape=...]
    unnamed x13 -> x0, local copies, waits for them, and re-layouts: 5.87 us -> none
where the time goes in v1:
time: 186 us
  Pallas kernels  185 us (99%)
    pallas_call x1, Pallas kernels, grid_step(): pl.pallas_call(functools.partial(grid_kernel, (full_width, owned, rank, s...  178 us
    pallas_call x1, Pallas kernels, grid_step(): pl.pallas_call(final_kernel, grid=(tokens_here // step_rows,), out_shape=...  6.64 us

profile of v1, /device:TPU:0, one launch (start us, length us, event | category | flops | bytes accessed | tf_op | source)
XLA Modules:
  0.0 185.5 jit_solution(3818420189250409145)
XLA Ops:
  0.6 178.3 %grid.1 = (f32[384,2816]{1,0:T(8,128)}, f32[384,128]{1,0:T(8,128)}, f32[384,128]{1,0:T(8,128)}, f32[3,16,2816]{2,1,0:T(8,128)}, f32[16,3072]{1,0:T(8,128)}, /*index=5*/f32[16,512]{1,0:T(8,128)}, f32[16,512]{1,0:T(8,128)}) custom-call(bf16[384,3072]{1,0:T(8,128)(2,1)} %cq.1, bf16[384,512]{1,0:T(8,128)(2,1)} %ck.1, bf16[384,512]{1,0:T(8,128)(2,1)} %cv.1, ...), custom_call_target="tpu_custom_call" | custom-call | flops 17716740096 | bytes 23068672 | tf_op jit(solution)/shard_map/grid/pallas_call | solution.py:688
  178.9 6.6 %final.1 = (bf16[384,2816]{1,0:T(8,128)(2,1)}, f32[3,16,2816]{2,1,0:T(8,128)}, f32[16,3072]{1,0:T(8,128)}, f32[16,512]{1,0:T(8,128)}, f32[16,512]{1,0:T(8,128)}) custom-call(f32[384,2816]{1,0:T(8,128)} %get-tuple-element.12.gained, bf16[384,2816]{1,0:T(8,128)(2,1)} %tokens.3, f32[384,128]{1,0:T(8,128)} %get-tuple-element.13.inner, ...), custom_call_target="tpu_custom_call" | custom-call | flops 4325376 | bytes 8650752 | tf_op jit(solution)/shard_map/final/pallas_call | solution.py:747

commit v2 on v1

--- a/solution.py
+++ b/solution.py
@@ -93,7 +93,7 @@
     out, inner_out, inverse_out, grad_down, grad_up_q, grad_up_k, grad_up_v,
     W, C, S, X, R,
     T, GW, GA, U, D, GD, A, AR, INV, LO, ZT, N, B, I, IR,
-    G, GC, GY, H, HZ, F,
+    G, GC, GY, H, HZ, F, GDV, GQ, GK, GV, grad_sem,
     load_w, load_c, load_s, store_sem,
     a_send, a_recv, i_send, i_recv,
     gc_send, gc_recv, gy_send, gy_recv, gz_send, gz_recv, ga_send, ga_recv, gb_send, gb_recv, gd_send, gd_recv,
@@ -577,13 +577,22 @@
     spread_c().wait_recv()
     for j in range(feature_blocks):
         for m in range(3):
-            grad_down[m, :, pl.ds(j * lanes, lanes)] = F[m * feature_blocks + j].astype(jnp.float32)
-    for m, ref in enumerate((grad_up_q, grad_up_k, grad_up_v)):
+            GDV[m, :, pl.ds(j * lanes, lanes)] = F[m * feature_blocks + j].astype(jnp.float32)
+    for m, ref in enumerate((GQ, GK, GV)):
         low, high = columns[m]
         for j in range((high - low) // lanes):
             ref[:, pl.ds(j * lanes, lanes)] = F[first + low // lanes + j].astype(jnp.float32)
     part = pl.ds(0, 3 * R.shape[1] // 4)
-    stores = []
+    stores = [
+        pltpu.make_async_copy(source, target, grad_sem.at[k])
+        for k, (source, target) in enumerate(
+            zip((GDV, GQ, GK, GV), (grad_down, grad_up_q, grad_up_k, grad_up_v))
+        )
+    ]
+    for i in range(count):
+        inverse_out[pl.ds(i * lanes, lanes), :] = INV[i]
+    for store in stores:
+        store.start()
     for i in range(count):
         rows = pl.ds(i * lanes, lanes)
         remote(R.at[i, part], R.at[i, part], r_send, r_recv.at[i], core).wait_recv()
@@ -600,7 +609,7 @@
             return carry + gained * (T[rows, cols].astype(jnp.float32) * inverse)
 
         total = lax.fori_loop(
-            0, feature_blocks, gained_block, jnp.zeros((lanes, lanes), jnp.float32), unroll=2
+            0, feature_blocks, gained_block, jnp.zeros((lanes, lanes), jnp.float32), unroll=11
         )
         I[i] = jnp.broadcast_to(jnp.sum(total, axis=1, keepdims=True), (lanes, lanes))
         inner_rows(i).start()
@@ -610,7 +619,6 @@
         rows = pl.ds(i * lanes, lanes)
         inner_rows(i).wait_recv()
         inner_out[rows, :] = (I[i] + IR[i]) / full_width
-        inverse_out[rows, :] = INV[i]
 
     results = remote(R.at[:, part], R.at[:, part], r_send, r_recv.at[0], core)
     results.wait_send()
@@ -694,7 +702,8 @@
             jax.ShapeDtypeStruct((3, rank, owned), f32),
         ) + tuple(jax.ShapeDtypeStruct((rank, c.shape[1]), f32) for c in cotangents),
         in_specs=[pl.BlockSpec(memory_space=pl.ANY)] * 12,
-        out_specs=(pl.BlockSpec(memory_space=pl.ANY),) + (vmem,) * 6,
+        out_specs=(pl.BlockSpec(memory_space=pl.ANY),) + (vmem,) * 2
+        + (pl.BlockSpec(memory_space=pl.ANY),) * 4,
         scratch_shapes=[
             pltpu.VMEM((8, half, depth), bf16),
             pltpu.VMEM((2 * count, 2 * lanes, depth), bf16),
@@ -722,6 +731,9 @@
             pltpu.VMEM((share // 2, rank, lanes), bf16),
             pltpu.VMEM((3, share // 8, rank, lanes), bf16),
             pltpu.VMEM((grad_blocks, rank, lanes), bf16),
+            pltpu.VMEM((3, rank, owned), f32),
+            *[pltpu.VMEM((rank, c.shape[1]), f32) for c in cotangents],
+            DMA((4,)),
             DMA((2, 3)), DMA((count, 3)), DMA((8,)), DMA((count,)),
             DMA, DMA, DMA, DMA((count,)),
             DMA, DMA, DMA, DMA, DMA, DMA((3,)), DMA, DMA((3,)), DMA, DMA, DMA, DMA,
@@ -738,7 +750,7 @@
         ),
         name="grid",
     )(*cotangents, *weights, tokens, gain.reshape(full_width // lanes, lanes), adapters, *ups)
-    step_rows = 64
+    step_rows = tokens_here // 2
 
     def by_rows(width):
         return pl.BlockSpec((step_rows, width), lambda i: (i, 0))

time: 186 us -> 182 us (0.978)
  Pallas kernels: 185 us -> 181 us
    pallas_call x1, Pallas kernels: 178 us -> 176 us  [grid_step(): pl.pallas_call(functools.partial(grid_kernel, (full_width, owned, rank, s...]
    pallas_call x1, Pallas kernels: 6.64 us -> 4.74 us  [grid_step(): pl.pallas_call(final_kernel, grid=(tokens_here // step_rows,), out_shape=...]
where the time goes in v2:
time: 182 us
  Pallas kernels  181 us (99%)
    pallas_call x1, Pallas kernels, grid_step(): pl.pallas_call(functools.partial(grid_kernel, (full_width, owned, rank, s...  176 us
    pallas_call x1, Pallas kernels, grid_step(): pl.pallas_call(final_kernel, grid=(tokens_here // step_rows,), out_shape=...  4.74 us

profile of v2, /device:TPU:0, one launch (start us, length us, event | category | flops | bytes accessed | tf_op | source)
XLA Modules:
  0.0 181.5 jit_solution(12990453908292256130)
XLA Ops:
  0.6 176.1 %grid.1 = (f32[384,2816]{1,0:T(8,128)}, f32[384,128]{1,0:T(8,128)}, f32[384,128]{1,0:T(8,128)}, f32[3,16,2816]{2,1,0:T(8,128)}, f32[16,3072]{1,0:T(8,128)}, /*index=5*/f32[16,512]{1,0:T(8,128)}, f32[16,512]{1,0:T(8,128)}) custom-call(bf16[384,3072]{1,0:T(8,128)(2,1)} %cq.1, bf16[384,512]{1,0:T(8,128)(2,1)} %ck.1, bf16[384,512]{1,0:T(8,128)(2,1)} %cv.1, ...), custom_call_target="tpu_custom_call" | custom-call | flops 17716740096 | bytes 23068672 | tf_op jit(solution)/shard_map/grid/pallas_call | solution.py:696
  176.8 4.7 %final.1 = (bf16[384,2816]{1,0:T(8,128)(2,1)}, f32[3,16,2816]{2,1,0:T(8,128)}, f32[16,3072]{1,0:T(8,128)}, f32[16,512]{1,0:T(8,128)}, f32[16,512]{1,0:T(8,128)}) custom-call(f32[384,2816]{1,0:T(8,128)} %get-tuple-element.12.gained, bf16[384,2816]{1,0:T(8,128)(2,1)} %tokens.3, f32[384,128]{1,0:T(8,128)} %get-tuple-element.13.inner, ...), custom_call_target="tpu_custom_call" | custom-call | flops 4325376 | bytes 8650752 | tf_op jit(solution)/shard_map/final/pallas_call | solution.py:759

commit v3 on v2

--- a/solution.py
+++ b/solution.py
@@ -404,7 +404,7 @@
         far_y(h, k).start()
 
     last_outer = f"z{count - 1}"
-    last_step = is_inner * inner_marks["f1"] + (1 - is_inner) * outer_marks[last_outer]
+    last_step = is_inner * inner_marks["f1"] + (1 - is_inner) * (outer_marks["fy1"] + 1)
     waiting = is_inner * count + (1 - is_inner) * (count - 1)
 
     def sum_rows(slot):
@@ -611,14 +611,15 @@
         total = lax.fori_loop(
             0, feature_blocks, gained_block, jnp.zeros((lanes, lanes), jnp.float32), unroll=11
         )
-        I[i] = jnp.broadcast_to(jnp.sum(total, axis=1, keepdims=True), (lanes, lanes))
+        I[i] = jnp.broadcast_to(jnp.sum(total.T, axis=0, keepdims=True), (8, lanes))
         inner_rows(i).start()
         stores.append(pltpu.make_async_copy(B.at[rows], out.at[rows], store_sem.at[i]))
         stores[-1].start()
     for i in range(count):
         rows = pl.ds(i * lanes, lanes)
         inner_rows(i).wait_recv()
-        inner_out[rows, :] = (I[i] + IR[i]) / full_width
+        inner = (I[i, pl.ds(0, 1)] + IR[i, pl.ds(0, 1)]) / full_width
+        inner_out[rows, :] = jnp.broadcast_to(inner, (lanes, lanes)).T
 
     results = remote(R.at[:, part], R.at[:, part], r_send, r_recv.at[0], core)
     results.wait_send()
@@ -723,8 +724,8 @@
             pltpu.VMEM((lanes, tokens_here), bf16),
             pltpu.VMEM((tokens_here, owned), bf16),
             pltpu.VMEM((tokens_here, owned), f32),
-            pltpu.VMEM((count, lanes, lanes), f32),
-            pltpu.VMEM((count, lanes, lanes), f32),
+            pltpu.VMEM((count, 8, lanes), f32),
+            pltpu.VMEM((count, 8, lanes), f32),
             pltpu.VMEM((grad_blocks, rank, lanes), f32),
             pltpu.VMEM((share, rank, lanes), f32),
             pltpu.VMEM((share // 2, rank, lanes), f32),

time: 182 us -> 180 us (0.989)
  Pallas kernels: 181 us -> 179 us
where the time goes in v3:
time: 180 us
  Pallas kernels  179 us (99%)
    pallas_call x1, Pallas kernels, grid_step(): pl.pallas_call(functools.partial(grid_kernel, (full_width, owned, rank, s...  175 us
    pallas_call x1, Pallas kernels, grid_step(): pl.pallas_call(final_kernel, grid=(tokens_here // step_rows,), out_shape=...  4.74 us

profile of v3, /device:TPU:0, one launch (start us, length us, event | category | flops | bytes accessed | tf_op | source)
XLA Modules:
  0.0 180.0 jit_solution(1694274094872590646)
XLA Ops:
  0.6 174.6 %grid.1 = (f32[384,2816]{1,0:T(8,128)}, f32[384,128]{1,0:T(8,128)}, f32[384,128]{1,0:T(8,128)}, f32[3,16,2816]{2,1,0:T(8,128)}, f32[16,3072]{1,0:T(8,128)}, /*index=5*/f32[16,512]{1,0:T(8,128)}, f32[16,512]{1,0:T(8,128)}) custom-call(bf16[384,3072]{1,0:T(8,128)(2,1)} %cq.1, bf16[384,512]{1,0:T(8,128)(2,1)} %ck.1, bf16[384,512]{1,0:T(8,128)(2,1)} %cv.1, ...), custom_call_target="tpu_custom_call" | custom-call | flops 17716740096 | bytes 23068672 | tf_op jit(solution)/shard_map/grid/pallas_call | solution.py:697
  175.2 4.7 %final.1 = (bf16[384,2816]{1,0:T(8,128)(2,1)}, f32[3,16,2816]{2,1,0:T(8,128)}, f32[16,3072]{1,0:T(8,128)}, f32[16,512]{1,0:T(8,128)}, f32[16,512]{1,0:T(8,128)}) custom-call(f32[384,2816]{1,0:T(8,128)} %get-tuple-element.12.gained, bf16[384,2816]{1,0:T(8,128)(2,1)} %tokens.3, f32[384,128]{1,0:T(8,128)} %get-tuple-element.13.inner, ...), custom_call_target="tpu_custom_call" | custom-call | flops 4325376 | bytes 8650752 | tf_op jit(solution)/shard_map/final/pallas_call | solution.py:760
